TPU v7x, 32 devices: a whole 2x2x4 slice. The times are simulated.
32 devices in a mesh: expert: 16 (over z, y, x), width: 2 (over core).
Axes of the slice: x: 2, y: 2, z: 4, core: 2. Of those that a mesh axis runs over, the one named last changes fastest.
Arguments:
- tokens: bfloat16 [1024, 6144], P('expert', 'width'), may hold values from -6 to 6
- expert_ids: int32 [1024, 8], P('expert'), may hold values from 0 to 383, all different within a row; in each aligned block of 64 rows (0 to 63, 64 to 127, ...) at most 2 rows name the same one
- route_weight: float32 [1024, 8], P('expert'), may hold values from 0.2 to 1.5
- gate_weight: bfloat16 [16, 6144, 1024], P('expert', None, 'width'), may hold values from -0.078125 to 0.078125
- up_weight: bfloat16 [16, 6144, 1024], P('expert', None, 'width'), may hold values from -0.078125 to 0.078125
- down_weight: bfloat16 [16, 6144, 1024], P('expert', None, 'width'), may hold values from -0.1875 to 0.1875
Outputs:
- mixed: bfloat16 [1024, 6144], P('expert', 'width')
Inputs may be any that keep to these rules, and one draw needn't show every extreme that they name: `expert_ids`: each row names 8 different experts. In each aligned block of 64 rows (the rows of one index of the expert axis) no expert is named by more than 2 rows.
All inputs are finite; a program needn't handle non-finite values.
Results may differ from a plain program's by a relative error of at most 0.014.
Values may be sent and summed in bfloat16 or wider, within the bound.
No kernel may reach another device: no remote copies, remote signals or barrier semaphores. Data moves between devices by JAX's collectives and lax.ppermute only.
A program may use at most 64 MiB of HBM per device.

v0:
```python
import jax
import jax.numpy as jnp
from jax import lax
from jax.sharding import PartitionSpec as P

SEND = 2


def local_slots(route_ids, holders):
    experts_held = jnp.arange(holders, dtype=jnp.int32)
    route_hits = route_ids[:, :, None] == experts_held[None, None, :]
    matched = jnp.any(route_hits, axis=1).astype(jnp.int32)
    ranking = jnp.cumsum(matched, axis=0) - matched
    return (route_hits, matched, ranking)


def body(tokens, expert_ids, route_weight, gate_weight, up_weight, down_weight):
    holders = lax.axis_size("expert")
    tok_rows = tokens.shape[0]
    capacity = holders * SEND
    route_hits, matched, ranking = local_slots(expert_ids, holders)
    expert_base = jnp.arange(holders, dtype=jnp.int32)[None, :] * SEND
    slot_of = jnp.where(matched > 0, expert_base + ranking, capacity)
    row_number = jnp.broadcast_to(jnp.arange(tok_rows, dtype=jnp.int32)[:, None], slot_of.shape)
    slot_table = (
        jnp.full((capacity + 1,), tok_rows, jnp.int32)
        .at[slot_of.reshape(-1)]
        .set(row_number.reshape(-1))
    )
    outgoing = jnp.take(tokens, slot_table[:capacity], axis=0, mode="fill", fill_value=0)
    arrived = lax.all_to_all(
        outgoing.reshape(holders, SEND, outgoing.shape[1]),
        "expert",
        split_axis=0,
        concat_axis=0,
        tiled=True,
    )
    selected = arrived.reshape(capacity, arrived.shape[2])
    gate_mat = gate_weight[0]
    up_mat = up_weight[0]
    down_mat = down_weight[0]
    segment = lax.all_gather(selected, "width", axis=1, tiled=True)
    gate_val = jnp.dot(segment, gate_mat, preferred_element_type=jnp.float32)
    up_val = jnp.dot(segment, up_mat, preferred_element_type=jnp.float32)
    hidden = (jax.nn.silu(gate_val) * up_val).astype(jnp.bfloat16)
    weights_held = jnp.sum(jnp.where(route_hits, route_weight[:, :, None], 0.0), axis=1)
    slot_onehot = (ranking[:, :, None] == jnp.arange(SEND, dtype=jnp.int32)[None, None, :]) & (
        matched[:, :, None] > 0
    )
    coeff = (weights_held[:, :, None] * slot_onehot.astype(jnp.float32)).reshape(tok_rows, capacity)
    feature_rows = down_mat.shape[0] // lax.axis_size("width")
    summed = lax.psum_scatter(
        lax.dot_general(
            down_mat, hidden, (((1,), (1,)), ((), ())), preferred_element_type=jnp.float32
        ).astype(jnp.bfloat16),
        "width",
        scatter_dimension=0,
        tiled=True,
    ).astype(jnp.float32)
    returned = lax.all_to_all(
        summed.reshape(feature_rows, holders, SEND).astype(jnp.bfloat16),
        "expert",
        split_axis=1,
        concat_axis=1,
        tiled=True,
    ).astype(jnp.float32)
    returned = returned.reshape(feature_rows, capacity)
    combined = lax.dot_general(
        coeff,
        returned,
        (((1,), (1,)), ((), ())),
        precision=lax.Precision.HIGHEST,
        preferred_element_type=jnp.float32,
    )
    return combined.astype(jnp.bfloat16)


def solution(mesh):
    in_specs = (
        P("expert", "width"),
        P("expert", None),
        P("expert", None),
        P("expert", None, "width"),
        P("expert", None, "width"),
        P("expert", None, "width"),
    )
    out_specs = P("expert", "width")
    return jax.shard_map(body, mesh=mesh, in_specs=in_specs, out_specs=out_specs, check_vma=False)
```

profile of v0, /device:TPU:0, one launch (start us, length us, event | category | flops | bytes accessed | tf_op | source)
XLA Modules:
  0.0 75.9 jit_solution(6627106244274575018)
XLA Ops:
  6.5 0.0 copy-start
  6.5 0.0 reduce-scatter.2.cloned.1.call-start
  6.5 0.8 fusion.21
  7.3 0.1 copy.22
  7.4 0.1 reshape.111
  7.5 0.1 reduce_window_sum.11
  7.6 0.1 select_n.44
  7.7 4.3 %scatter_custom_fusion = s32[33]{0:T(128)S(1)} fusion(s32[1024]{0:T(1024)S(1)} %bitcast.27, s32[1024]{0:T(1024)S(1)} %reshape.111, s32[]{:T(128)} %constant.14.clone.1), kind=kCustom, calls=%fused_computation.40 | custom fusion | bytes 136 | tf_op jit(solution)/shard_map/scatter | solution.py:28
  12.0 0.1 slice.6
  12.1 0.0 copy-done
  12.2 0.7 gather_fusion
  12.8 0.1 gather.7
  12.9 0.3 broadcast_select_fusion
  13.2 16.8 %all_to_all.10 = bf16[16,2,3072]{2,1,0:T(2,128)(2,1)S(1)} all-to-all(bf16[16,2,3072]{2,1,0:T(2,128)(2,1)S(1)} %broadcast_select_fusion), channel_id=1, replica_groups=mesh['expert'=16,'width'=2] {'expert'}, dimensions={0} | all-to-all | bytes 393216 | tf_op jit(solution)/shard_map/all_to_all | solution.py:31
  30.0 0.1 reshape.98
  30.0 2.1 %all_gather.3 = bf16[32,6144]{1,0:T(8,128)(2,1)S(1)} all-gather(bf16[32,3072]{1,0:T(8,128)(2,1)S(1)} %reshape.98), channel_id=1, replica_groups=mesh['expert'=16,'width'=2] {'width'}, dimensions={1}, use_global_device_ids=true | all-gather | bytes 589824 | tf_op jit(solution)/shard_map/all_gather | solution.py:42
  32.1 3.9 %fusion.4 = f32[32,512]{1,0:T(8,128)S(1)} fusion(bf16[32,6144]{1,0:T(8,128)(2,1)S(1)} %all_gather.3, bf16[1,6144,512]{2,1,0:T(8,128)(2,1)} %param.9), kind=kOutput, calls=%fused_computation.7 | convolution fusion | flops 201326592 | bytes 6750208 | tf_op jit(solution)/shard_map/dot_general | solution.py:43
  36.1 0.0 copy-start.1
  36.1 0.0 copy-start.2
  36.1 8.4 %fusion = bf16[6144,32]{0,1:T(8,128)(2,1)} fusion(bf16[1,6144,512]{2,1,0:T(8,128)(2,1)} %param.11, bf16[32,6144]{1,0:T(8,128)(2,1)S(1)} %all_gather.3, bf16[1,6144,512]{2,1,0:T(8,128)(2,1)} %param.10, f32[32,512]{1,0:T(8,128)S(1)} %fusion.4), kind=kOutput, calls=%fused_computation.3 | convolution fusion | flops 402948096 | bytes 13434880 | tf_op jit(solution)/shard_map/dot_general | solution.py:53
  44.5 0.0 reduce-scatter.2.cloned.1.call-update
  44.5 5.7 %reduce-scatter.2.cloned.1.call-done = bf16[3072,32]{0,1:T(8,128)(2,1)} async-done(((bf16[6144,32]{0,1:T(8,128)(2,1)}), bf16[3072,32]{0,1:T(8,128)(2,1)}) %reduce-scatter.2.cloned.1.call-update) | async-done | bytes 196624 | tf_op jit(solution)/shard_map/reduce_scatter | solution.py:52
  50.2 1.7 %convert_element_type.42 = bf16[3072,16,2]{0,2,1:T(2,128)(2,1)} reshape(bf16[3072,32]{0,1:T(8,128)(2,1)} %reduce-scatter.2.cloned.1.call-done) | data formatting | bytes 393216 | tf_op jit(solution)/shard_map/convert_element_type | solution.py:61
  51.9 6.7 %all-to-all-start.1 = ((bf16[3072,16,2]{0,2,1:T(2,128)(2,1)}), bf16[3072,16,2]{0,2,1:T(2,128)(2,1)S(1)}, u32[]{:S(2)}, u32[]{:S(2)}) async-start(bf16[3072,16,2]{0,2,1:T(2,128)(2,1)} %convert_element_type.42), calls=%async_computation.2 | async-start | bytes 393216 | tf_op jit(solution)/shard_map/all_to_all | solution.py:60
  58.7 0.1 copy.24
  58.7 0.1 copy.23
  58.8 0.0 copy-done.1
  58.8 0.0 copy-done.2
  58.9 9.0 %all-to-all-done.1 = bf16[3072,16,2]{0,2,1:T(2,128)(2,1)S(1)} async-done(((bf16[3072,16,2]{0,2,1:T(2,128)(2,1)}), bf16[3072,16,2]{0,2,1:T(2,128)(2,1)S(1)}, u32[]{:S(2)}, u32[]{:S(2)}) %all-to-all-start.1) | async-done | bytes 196640 | tf_op jit(solution)/shard_map/all_to_all | solution.py:60
  67.8 1.3 %fusion.6 = bf16[64,3072]{1,0:T(8,128)(2,1)} fusion(bf16[3072,16,2]{0,2,1:T(2,128)(2,1)S(1)} %all-to-all-done.1, f32[64,16]{0,1:T(8,128)S(1)} %select_reduce_fusion, s32[64,16]{0,1:T(8,128)S(1)} %copy.23, pred[64,16]{0,1:T(8,128)(4,1)S(1)} %copy.24), kind=kOutput, calls=%fused_computation.10 | convolution fusion | flops 75700224 | bytes 599040 | tf_op jit(solution)/shard_map/dot_general | solution.py:68
  (9 shorter events, 0.1 us)
Async XLA Ops:
  6.5 5.6 %copy-start = (bf16[64,3072]{1,0:T(8,128)(2,1)S(1)}, bf16[64,3072]{1,0:T(8,128)(2,1)}, u32[]{:S(2)}) copy-start(bf16[64,3072]{1,0:T(8,128)(2,1)} %param.6) | copy-start | bytes 1179652
  6.5 43.7 %reduce-scatter.2.cloned.1.call-start = ((), (), s32[]{:S(2)}) async-start(), calls=%async_computation.3 | async-start | bytes 589824 | tf_op jit(solution)/shard_map/reduce_scatter | solution.py:52
  36.1 22.7 %copy-start.1 = (s32[64,8]{0,1:T(8,128)S(1)}, s32[64,8]{0,1:T(8,128)}, u32[]{:S(2)}) copy-start(s32[64,8]{0,1:T(8,128)} %param.7) | copy-start | bytes 6148
  36.1 22.7 %copy-start.2 = (f32[64,8]{0,1:T(8,128)S(1)}, f32[64,8]{0,1:T(8,128)}, u32[]{:S(2)}) copy-start(f32[64,8]{0,1:T(8,128)} %param.8) | copy-start | bytes 6148
  51.9 15.9 %all-to-all-start.1 = ((bf16[3072,16,2]{0,2,1:T(2,128)(2,1)}), bf16[3072,16,2]{0,2,1:T(2,128)(2,1)S(1)}, u32[]{:S(2)}, u32[]{:S(2)}) async-start(bf16[3072,16,2]{0,2,1:T(2,128)(2,1)} %convert_element_type.42), calls=%async_computation.2 | async-start | bytes 393216 | tf_op jit(solution)/shard_map/all_to_all | solution.py:60
Sparse Core Ops, SparseCore 0:
  44.6 5.5 reduce-scatter.1
where the time goes:
time: 76.2 us; the launch traced here: 75.9 us
  blocking collectives  18.9 us (25%)
  waiting for transfers between devices  14.7 us (19%)
  matrix products  13.6 us (18%)
  between operations  13.5 us (18%)
  local copies, waits for them, and re-layouts  7.31 us (10%)
  starting transfers between devices  6.74 us (9%)
  other arithmetic  1.2 us (2%)
    all_to_all x1, blocking collectives, body(): lax.all_to_all(outgoing.reshape(holders, SEND, outgoing.shape[1]), 'exper...  16.8 us
    all_to_all x1, waiting for transfers between devices, body(): lax.all_to_all(summed.reshape(feature_rows, holders, SEND).astype(jnp.bfl...  8.96 us
    dot_general x1, matrix products, body(): lax.dot_general(down_mat, hidden, (((1,), (1,)), ((), ())), preferred_ele...  8.41 us
    all_to_all x1, starting transfers between devices, body(): lax.all_to_all(summed.reshape(feature_rows, holders, SEND).astype(jnp.bfl...  6.74 us
    reduce_scatter x1, waiting for transfers between devices, body(): lax.psum_scatter(lax.dot_general(down_mat, hidden, (((1,), (1,)), ((), ()...  5.72 us
    scatter x1, local copies, waits for them, and re-layouts, body(): slot_table = jnp.full((capacity + 1,), tok_rows, jnp.int32).at[slot_of.re...  4.3 us
    dot_general x1, matrix products, body(): gate_val = jnp.dot(segment, gate_mat, preferred_element_type=jnp.float32)  3.94 us
    all_gather x1, blocking collectives, body(): segment = lax.all_gather(selected, 'width', axis=1, tiled=True)  2.09 us
  transfers between devices with their start and end apart: 2, of which 2 were waited for; matrix products, arithmetic and copies ran while one was open for 0% of the time, Pallas kernels for 0%

commit v1 on v0

--- a/solution.py
+++ b/solution.py
@@ -57,12 +57,20 @@
         scatter_dimension=0,
         tiled=True,
     ).astype(jnp.float32)
-    returned = lax.all_to_all(
-        summed.reshape(feature_rows, holders, SEND).astype(jnp.bfloat16),
-        "expert",
-        split_axis=1,
-        concat_axis=1,
-        tiled=True,
+    returned = jnp.concatenate(
+        lax.all_to_all(
+            jnp.stack(
+                jnp.split(
+                    summed.reshape(feature_rows, holders, SEND).astype(jnp.bfloat16),
+                    lax.axis_size("expert"),
+                    axis=1,
+                )
+            ),
+            "expert",
+            0,
+            0,
+        ),
+        axis=1,
     ).astype(jnp.float32)
     returned = returned.reshape(feature_rows, capacity)
     combined = lax.dot_general(

time: 76.2 us -> 85.4 us (1.12)
  local copies, waits for them, and re-layouts: 7.31 us -> 16.4 us
    unnamed x6 -> x21, local copies, waits for them, and re-layouts: 0.02 us -> 9.16 us
where the time goes in v1:
time: 85.4 us; the launch traced here: 85.1 us
  blocking collectives  18.9 us (22%)
  local copies, waits for them, and re-layouts  16.4 us (19%)
  waiting for transfers between devices  14.7 us (17%)
  matrix products  13.6 us (16%)
  between operations  13.5 us (16%)
  starting transfers between devices  6.74 us (8%)
  other arithmetic  1.22 us (1%)
    all_to_all x1, blocking collectives, body(): lax.all_to_all(outgoing.reshape(holders, SEND, outgoing.shape[1]), 'exper...  16.8 us
    unnamed x21, local copies, waits for them, and re-layouts  9.16 us
    all_to_all x1, waiting for transfers between devices, body(): lax.all_to_all(jnp.stack(jnp.split(summed.reshape(feature_rows, holders,...  8.93 us
    dot_general x1, matrix products, body(): lax.dot_general(down_mat, hidden, (((1,), (1,)), ((), ())), preferred_ele...  8.41 us
    all_to_all x1, starting transfers between devices, body(): lax.all_to_all(jnp.stack(jnp.split(summed.reshape(feature_rows, holders,...  6.74 us
    reduce_scatter x1, waiting for transfers between devices, body(): lax.psum_scatter(lax.dot_general(down_mat, hidden, (((1,), (1,)), ((), ()...  5.72 us
    scatter x1, local copies, waits for them, and re-layouts, body(): slot_table = jnp.full((capacity + 1,), tok_rows, jnp.int32).at[slot_of.re...  4.3 us
    dot_general x1, matrix products, body(): gate_val = jnp.dot(segment, gate_mat, preferred_element_type=jnp.float32)  3.94 us
  transfers between devices with their start and end apart: 2, of which 2 were waited for; matrix products, arithmetic and copies ran while one was open for 0% of the time, Pallas kernels for 0%

profile of v1, /device:TPU:0, one launch (start us, length us, event | category | flops | bytes accessed | tf_op | source)
XLA Modules:
  0.0 85.1 jit_solution(1261917490522471496)
XLA Ops:
  6.5 0.8 fusion.19
  7.3 0.1 copy.13
  7.5 0.1 reduce_window_sum.11
  7.6 0.1 select_n.44
  7.7 4.3 %scatter_custom_fusion = s32[33]{0:T(128)S(1)} fusion(s32[1024]{0:T(1024)S(1)} %bitcast.95, s32[1024]{0:T(1024)S(1)} %reshape.160, s32[]{:T(128)} %constant.14.clone.1), kind=kCustom, calls=%fused_computation.64 | custom fusion | bytes 136 | tf_op jit(solution)/shard_map/scatter | solution.py:28
  12.2 0.7 gather_fusion
  12.9 0.3 broadcast_select_fusion
  13.2 16.8 %all_to_all.10 = bf16[16,2,3072]{2,1,0:T(2,128)(2,1)S(1)} all-to-all(bf16[16,2,3072]{2,1,0:T(2,128)(2,1)S(1)} %broadcast_select_fusion), channel_id=1, replica_groups=mesh['expert'=16,'width'=2] {'expert'}, dimensions={0} | all-to-all | bytes 393216 | tf_op jit(solution)/shard_map/all_to_all | solution.py:31
  30.0 2.1 %all_gather.3 = bf16[32,6144]{1,0:T(8,128)(2,1)S(1)} all-gather(bf16[32,3072]{1,0:T(8,128)(2,1)S(1)} %reshape.145), channel_id=1, replica_groups=mesh['expert'=16,'width'=2] {'width'}, dimensions={1}, use_global_device_ids=true | all-gather | bytes 589824 | tf_op jit(solution)/shard_map/all_gather | solution.py:42
  32.1 3.9 %fusion.4 = f32[32,512]{1,0:T(8,128)S(1)} fusion(bf16[32,6144]{1,0:T(8,128)(2,1)S(1)} %all_gather.3, bf16[1,6144,512]{2,1,0:T(8,128)(2,1)} %param.9), kind=kOutput, calls=%fused_computation.7 | convolution fusion | flops 201326592 | bytes 6750208 | tf_op jit(solution)/shard_map/dot_general | solution.py:43
  36.1 8.4 %fusion = bf16[6144,32]{0,1:T(8,128)(2,1)} fusion(bf16[1,6144,512]{2,1,0:T(8,128)(2,1)} %param.11, bf16[32,6144]{1,0:T(8,128)(2,1)S(1)} %all_gather.3, bf16[1,6144,512]{2,1,0:T(8,128)(2,1)} %param.10, f32[32,512]{1,0:T(8,128)S(1)} %fusion.4), kind=kOutput, calls=%fused_computation.3 | convolution fusion | flops 402948096 | bytes 13434880 | tf_op jit(solution)/shard_map/dot_general | solution.py:53
  44.5 5.7 %reduce-scatter.2.cloned.1.call-done = bf16[3072,32]{0,1:T(8,128)(2,1)} async-done(((bf16[6144,32]{0,1:T(8,128)(2,1)}), bf16[3072,32]{0,1:T(8,128)(2,1)}) %reduce-scatter.2.cloned.1.call-update) | async-done | bytes 196624 | tf_op jit(solution)/shard_map/reduce_scatter | solution.py:52
  50.2 1.0 %convert_element_type.42 = bf16[3072,16,2]{0,2,1:T(2,128)(2,1)S(1)} reshape(bf16[3072,32]{0,1:T(8,128)(2,1)} %reduce-scatter.2.cloned.1.call-done) | data formatting | bytes 393216 | tf_op jit(solution)/shard_map/convert_element_type | solution.py:64
  51.2 0.6 constant_dynamic-update-slice_fusion.15
  51.9 0.6 constant_dynamic-update-slice_fusion.14
  52.5 0.6 constant_dynamic-update-slice_fusion.13
  53.1 0.6 constant_dynamic-update-slice_fusion.12
  53.7 0.6 constant_dynamic-update-slice_fusion.11
  54.3 0.6 constant_dynamic-update-slice_fusion.10
  54.9 0.6 constant_dynamic-update-slice_fusion.9
  55.5 0.6 constant_dynamic-update-slice_fusion.8
  56.1 0.6 constant_dynamic-update-slice_fusion.7
  56.7 0.6 constant_dynamic-update-slice_fusion.6
  57.3 0.6 constant_dynamic-update-slice_fusion.5
  58.0 0.6 constant_dynamic-update-slice_fusion.4
  58.6 0.6 constant_dynamic-update-slice_fusion.3
  59.2 0.6 constant_dynamic-update-slice_fusion.2
  59.8 0.6 constant_dynamic-update-slice_fusion.1
  60.4 0.6 constant_dynamic-update-slice_fusion
  61.0 6.7 %all-to-all-start.1 = ((bf16[16,3072,1,2]{1,3,2,0:T(2,128)(2,1)}), bf16[16,3072,1,2]{1,3,2,0:T(2,128)(2,1)S(1)}, u32[]{:S(2)}, u32[]{:S(2)}) async-start(bf16[16,3072,1,2]{1,3,2,0:T(2,128)(2,1)} %constant_dynamic-update-slice_fusion), calls=%async_computation.2 | async-start | bytes 393216 | tf_op jit(solution)/shard_map/all_to_all | solution.py:61
  68.0 8.9 %all-to-all-done.1 = bf16[16,3072,1,2]{1,3,2,0:T(2,128)(2,1)S(1)} async-done(((bf16[16,3072,1,2]{1,3,2,0:T(2,128)(2,1)}), bf16[16,3072,1,2]{1,3,2,0:T(2,128)(2,1)S(1)}, u32[]{:S(2)}, u32[]{:S(2)}) %all-to-all-start.1) | async-done | bytes 196640 | tf_op jit(solution)/shard_map/all_to_all | solution.py:61
  77.0 1.3 %convolution_convert_fusion.1 = bf16[64,3072]{1,0:T(8,128)(2,1)} fusion(f32[64,32]{0,1:T(8,128)S(1)} %bitcast.94, bf16[3072,32]{0,1:T(8,128)(2,1)S(1)} %reshape.147), kind=kOutput, calls=%fused_computation.9 | convolution fusion | flops 75694080 | bytes 598016 | tf_op jit(solution)/shard_map/dot_general | solution.py:76
  (25 shorter events, 0.7 us)
Async XLA Ops:
  6.5 5.6 %copy-start = (bf16[64,3072]{1,0:T(8,128)(2,1)S(1)}, bf16[64,3072]{1,0:T(8,128)(2,1)}, u32[]{:S(2)}) copy-start(bf16[64,3072]{1,0:T(8,128)(2,1)} %param.6) | copy-start | bytes 1179652
  6.5 43.7 %reduce-scatter.2.cloned.1.call-start = ((), (), s32[]{:S(2)}) async-start(), calls=%async_computation.3 | async-start | bytes 589824 | tf_op jit(solution)/shard_map/reduce_scatter | solution.py:52
  36.1 31.8 %copy-start.1 = (s32[64,8]{0,1:T(8,128)S(1)}, s32[64,8]{0,1:T(8,128)}, u32[]{:S(2)}) copy-start(s32[64,8]{0,1:T(8,128)} %param.7) | copy-start | bytes 6148
  36.1 31.8 %copy-start.2 = (f32[64,8]{0,1:T(8,128)S(1)}, f32[64,8]{0,1:T(8,128)}, u32[]{:S(2)}) copy-start(f32[64,8]{0,1:T(8,128)} %param.8) | copy-start | bytes 6148
  61.0 15.9 %all-to-all-start.1 = ((bf16[16,3072,1,2]{1,3,2,0:T(2,128)(2,1)}), bf16[16,3072,1,2]{1,3,2,0:T(2,128)(2,1)S(1)}, u32[]{:S(2)}, u32[]{:S(2)}) async-start(bf16[16,3072,1,2]{1,3,2,0:T(2,128)(2,1)} %constant_dynamic-update-slice_fusion), calls=%async_computation.2 | async-start | bytes 393216 | tf_op jit(solution)/shard_map/all_to_all | solution.py:61
Sparse Core Ops, SparseCore 0:
  44.6 5.5 reduce-scatter.1
